TPU v7x, 128 devices: a whole 4x4x4 slice. The times are simulated.
128 devices in a mesh: seq: 8 (over z, core), grp: 16 (over y, x).
Axes of the slice: x: 4, y: 4, z: 4, core: 2. Of those that a mesh axis runs over, the one named last changes fastest.
Arguments:
- hidden_in: bfloat16 [16, 4096, 1024], P('grp', 'seq'), may hold values from -64 to 64, as said below
- lengths: int32 [16], P('grp'), may hold values from 512 to 4096
- project_weight: bfloat16 [1024, 3072], replicated, may hold values from -0.1875 to 0.1875
- output_weight: bfloat16 [1024, 1024], replicated, may hold values from -0.1875 to 0.1875
- first_gain: float32 [1024], replicated, may hold values from 0.5 to 1.5
- first_shift: float32 [1024], replicated, may hold values from -3 to 3
- up_weight: bfloat16 [1024, 4096], P('grp'), may hold values from -0.1875 to 0.1875
- down_weight: bfloat16 [1024, 4096], P('grp'), may hold values from -0.09375 to 0.09375
- second_gain: float32 [1024], replicated, may hold values from 0.5 to 1.5
- second_shift: float32 [1024], replicated, may hold values from -3 to 3
- queries: float32 [128, 1024], P('grp'), may hold values from -6 to 6
- positive: int32 [128], P('grp'), may hold values from 0 to 15
Outputs:
- hidden_out: bfloat16 [16, 4096, 1024], P('grp', 'seq')
- embeddings: float32 [16, 1024], P('grp')
- query_loss: float32 [128], P('grp')
Inputs may be any that keep to these rules, and one draw needn't show every extreme that they name: `hidden_in`: activations.
All inputs are finite; a program needn't handle non-finite values.
Results may differ from a plain program's by a relative error of at most 0.0076.
Values may be sent and summed in bfloat16 or wider, within the bound.
A program may use at most 192 MiB of HBM per device.

v0:
```python
import math

import jax
import jax.numpy as jnp
from jax import lax
from jax.sharding import PartitionSpec as P

HEAD_DIM = 64


def sent_together(arrays, axis, dim, along):
    widths = [a.shape[along] for a in arrays]
    both = jnp.concatenate(arrays, axis=along)
    result = lax.all_gather(both, axis, axis=dim, tiled=True)
    return tuple(jnp.split(result, [sum(widths[:k]) for k in range(1, len(widths))], axis=along))


def split_up(array, dim, devices):
    before, after = (array.shape[:dim], array.shape[dim + 1 :])
    return jnp.moveaxis(array.reshape(*before, devices, -1, *after), dim, 0)


def cut_rows(length, count):
    unit = 8 if length >= 8 * count else 1
    return [length // unit * k // count * unit for k in range(1, count)]


def laid_out(parts, dim):
    lengths = list(parts.shape[1:])
    lengths[dim] *= parts.shape[0]
    return jnp.moveaxis(parts, 0, dim).reshape(lengths)


def several_exchanges(array, axis, pieces, split_dim, concat_dim):
    parts = split_up(array, split_dim, lax.axis_size(axis))
    cut = max(range(1, max(2, parts.ndim - 1)), key=lambda d: parts.shape[d])
    outs = []
    for slab in jnp.split(parts, cut_rows(parts.shape[cut], pieces), axis=cut):
        if slab.size:
            outs.append(lax.all_to_all(slab, axis, split_axis=0, concat_axis=0, tiled=True))
    return laid_out(jnp.concatenate(outs, axis=cut), concat_dim)


def sent_to_all(array, axis):
    copies = jnp.broadcast_to(array, (lax.axis_size(axis), *array.shape))
    return lax.all_to_all(copies, axis, split_axis=0, concat_axis=0, tiled=True)


def taken_together(array, axis):
    everything = sent_to_all(array, axis)
    return jnp.sum(everything, axis=0)


def collect(array, axis, dim):
    parts = sent_to_all(array, axis)
    return laid_out(parts, dim)


def layer_norm(values, gain, shift):
    average = jnp.mean(values, axis=-1, keepdims=True)
    centred = values - average
    variance = jnp.mean(centred * centred, axis=-1, keepdims=True)
    return centred * lax.rsqrt(variance + 1e-05) * gain + shift


def attend_local(gathered, length):
    seq_len = gathered.shape[0]
    local_width = gathered.shape[2]
    head_count = local_width // HEAD_DIM
    block = min(1024, seq_len)
    query_all = gathered[:, 0, :].reshape(seq_len, head_count, HEAD_DIM)
    key_all = gathered[:, 1, :].reshape(seq_len, head_count, HEAD_DIM)
    value_all = gathered[:, 2, :].reshape(seq_len, head_count, HEAD_DIM)
    key_valid = jnp.arange(seq_len, dtype=jnp.int32) < length
    scale = 1.0 / math.sqrt(HEAD_DIM)

    def one_block(index):
        query_rows = lax.dynamic_slice_in_dim(query_all, index * block, block, 0)
        scores = (
            jnp.einsum("qhd,khd->hqk", query_rows, key_all, preferred_element_type=jnp.float32)
            * scale
        )
        scores = jnp.where(key_valid[None, None, :], scores, -jnp.inf)
        highest = jnp.max(scores, axis=-1, keepdims=True)
        expo = jnp.exp(scores - highest)
        probs = (expo / jnp.sum(expo, axis=-1, keepdims=True)).astype(jnp.bfloat16)
        result = jnp.einsum("hqk,khd->qhd", probs, value_all, preferred_element_type=jnp.float32)
        return result.astype(jnp.bfloat16).reshape(block, local_width)

    blocks = lax.map(one_block, jnp.arange(seq_len // block, dtype=jnp.int32))
    return blocks.reshape(seq_len, local_width)


def group_weights(up_part, down_part):
    return sent_together((up_part, down_part), "grp", 0, 1)


def expand_inner(rows_in, up_full):
    return jax.nn.gelu(
        jnp.dot(rows_in, up_full, preferred_element_type=jnp.float32), approximate=False
    ).astype(jnp.bfloat16)


def contract_down(inner_rows, down_full):
    return lax.dot_general(
        inner_rows, down_full, (((1,), (1,)), ((), ())), preferred_element_type=jnp.float32
    )


def body(
    hidden_in,
    lengths,
    project_weight,
    output_weight,
    first_gain,
    first_shift,
    up_weight,
    down_weight,
    second_gain,
    second_shift,
    queries,
    positive,
):
    tokens = hidden_in[0]
    tok_rows = tokens.shape[0]
    width = tokens.shape[1]
    rank = lax.axis_index("seq")
    length = lengths[0]
    projected = jnp.dot(tokens, project_weight, preferred_element_type=jnp.float32).astype(
        jnp.bfloat16
    )
    projected = projected.reshape(tok_rows, 3, width)
    gathered = several_exchanges(projected, "seq", 2, 2, 0)
    attended = attend_local(gathered, length)
    returned = lax.all_to_all(attended, "seq", split_axis=0, concat_axis=1, tiled=True)
    mixed = jnp.dot(returned, output_weight, preferred_element_type=jnp.float32)
    mixed = mixed + tokens.astype(jnp.float32)
    normed = layer_norm(mixed, first_gain, first_shift).astype(jnp.bfloat16)
    up_full, down_full = group_weights(up_weight, down_weight)
    inner = expand_inner(normed, up_full)
    outer = contract_down(inner, down_full)
    final = layer_norm(outer + normed.astype(jnp.float32), second_gain, second_shift)
    position = rank * tok_rows + jnp.arange(tok_rows, dtype=jnp.int32)
    valid = (position < length).astype(jnp.float32)
    local_total = jnp.sum(final * valid[:, None], axis=0)
    passage_total = taken_together(local_total, "seq")
    pooled = passage_total / length.astype(jnp.float32)
    embedding = pooled / jnp.sqrt(jnp.sum(pooled * pooled) + 1e-06)
    short_passages = collect(embedding.astype(jnp.bfloat16)[None, :], "grp", 0)
    short_queries = (
        queries / jnp.sqrt(jnp.sum(queries * queries, axis=-1, keepdims=True) + 1e-06)
    ).astype(jnp.bfloat16)
    logits = 20.0 * jnp.dot(short_queries, short_passages.T, preferred_element_type=jnp.float32)
    passage_ids = jnp.arange(short_passages.shape[0], dtype=jnp.int32)
    chosen = positive[:, None] == passage_ids[None, :]
    picked = jnp.sum(jnp.where(chosen, logits, 0.0), axis=1)
    query_loss = jnp.log(jnp.sum(jnp.exp(logits), axis=1)) - picked
    return (final.astype(jnp.bfloat16)[None], embedding[None, :], query_loss)


def solution(mesh):
    in_specs = (
        P("grp", "seq", None),
        P("grp"),
        P(),
        P(),
        P(),
        P(),
        P("grp", None),
        P("grp", None),
        P(),
        P(),
        P("grp", None),
        P("grp"),
    )
    out_specs = (P("grp", "seq", None), P("grp", None), P("grp"))
    return jax.shard_map(body, mesh=mesh, in_specs=in_specs, out_specs=out_specs, check_vma=False)
```

profile of v0, /device:TPU:1, one launch (start us, length us, event | category | flops | bytes accessed | tf_op | source)
XLA Modules:
  0.0 312.9 jit_solution(6332534830161004990)
XLA Ops:
  7.2 0.0 all-gather.2.cloned.1.call-start
  7.2 2.4 pad_maximum_fusion.1
  9.6 6.6 %fusion.69 = bf16[64,8,24,128]{3,1,2,0:T(8,128)(2,1)S(1)} fusion(bf16[1024,3072]{1,0:T(8,128)(2,1)} %param.16, bf16[1,512,1024]{2,1,0:T(8,128)(2,1)} %param.14), kind=kOutput, calls=%fused_computation.84 | convolution fusion | flops 3222798336 | bytes 10485760 | tf_op jit(solution)/shard_map/dot_general | solution.py:129
  16.2 0.9 copy.57
  17.1 0.7 copy.65
  17.7 1.5 fusion.130
  19.3 27.2 %all_to_all.40 = bf16[8,256,3,128]{3,1,2,0:T(8,128)(2,1)} all-to-all(bf16[8,256,3,128]{3,1,2,0:T(8,128)(2,1)S(1)} %get-tuple-element.88), channel_id=1, replica_groups=mesh['seq'=8,'grp'=16] {'seq'}, dimensions={0} | all-to-all | bytes 3145728 | tf_op jit(solution)/shard_map/all_to_all | solution.py:40
  46.5 5.2 %all-to-all-start.1 = ((bf16[8,256,3,128]{3,1,2,0:T(8,128)(2,1)}), bf16[8,256,3,128]{3,1,2,0:T(8,128)(2,1)}, u32[]{:S(2)}, u32[]{:S(2)}) async-start(bf16[8,256,3,128]{3,1,2,0:T(8,128)(2,1)} %get-tuple-element.89), calls=%async_computation.1 | async-start | bytes 3145728 | tf_op jit(solution)/shard_map/all_to_all | solution.py:40
  51.7 20.7 %all-to-all-done.1 = bf16[8,256,3,128]{3,1,2,0:T(8,128)(2,1)} async-done(((bf16[8,256,3,128]{3,1,2,0:T(8,128)(2,1)}), bf16[8,256,3,128]{3,1,2,0:T(8,128)(2,1)}, u32[]{:S(2)}, u32[]{:S(2)}) %all-to-all-start.1) | async-done | bytes 1572896 | tf_op jit(solution)/shard_map/all_to_all | solution.py:40
  72.4 2.2 pad_maximum_fusion
  74.6 0.3 copy.52
  74.9 1.6 fusion.129
  76.5 2.3 copy.46
  78.8 2.3 copy.47
  81.1 1.3 copy.48
  82.4 134.7 %while.11 = (s32[]{:T(128)}, bf16[4,1024,128]{2,1,0:T(8,128)(2,1)}, s32[4]{0:T(128)S(1)}, bf16[4096,2,64]{0,2,1:T(8,128)(2,1)}, bf16[4096,2,64]{0,2,1:T(8,128)(2...) while((s32[]{:T(128)}, bf16[4,1024,128]{2,1,0:T(8,128)(2,1)}, ...), condition=%wide.region_3.4_spmd.clone, body=%wide.region_0.3_spmd.clone.sunk | while | flops 2197954560 | bytes 70804144 | solution.py:90
  82.4 0.6 dynamic_slice.24
  83.6 0.7 iota_compare_fusion.3
  84.3 17.5 %fusion.154 = (f32[2,1024]{1,0:T(2,128)S(1)}, f32[2,1024,4096]{2,1,0:T(8,128)}) fusion(pred[4096]{0:T(1024)(128)(4,1)S(1)} %iota_compare_fusion.3, bf16[4096,2,64]{0,2,1:T(8,128)(2,1)} %get-tuple-element.169, bf16[4096,2,64]{0,2,1:T(8,128)(2,1)} %get-tuple-element.168, s32[]{:T(128)S(6)} %select_n.28), kind=kOutput, calls=%fused_computation.143.clone.1 | convolution fusion | flops 1107300352 | bytes 34877444 | tf_op jit(solution)/shard_map/while/body/eval_jaxpr/sub | solution.py:85
  101.8 13.9 %fusion.155 = bf16[2,1024,64]{1,2,0:T(8,128)(2,1)S(1)} fusion(bf16[4096,2,64]{0,2,1:T(8,128)(2,1)} %get-tuple-element.170, f32[2,1024,4096]{2,1,0:T(8,128)} %get-tuple-element.141, f32[2,1024]{1,0:T(2,128)S(1)} %get-tuple-element.142), kind=kOutput, calls=%fused_computation.11.clone.1 | convolution fusion | flops 1090650112 | bytes 34873344 | tf_op jit(solution)/shard_map/while/body/eval_jaxpr/hqk,khd->qhd/dot_general | solution.py:87
  115.7 0.2 copy.67
  115.9 0.7 constant_dynamic-update-slice_fusion.2
  116.6 0.6 dynamic_slice.24
  117.9 0.7 iota_compare_fusion.3
  118.5 17.1 %fusion.154 = (f32[2,1024]{1,0:T(2,128)S(1)}, f32[2,1024,4096]{2,1,0:T(8,128)}) fusion(pred[4096]{0:T(1024)(128)(4,1)S(1)} %iota_compare_fusion.3, bf16[4096,2,64]{0,2,1:T(8,128)(2,1)} %get-tuple-element.169, bf16[4096,2,64]{0,2,1:T(8,128)(2,1)} %get-tuple-element.168, s32[]{:T(128)S(6)} %select_n.28), kind=kOutput, calls=%fused_computation.143.clone.1 | convolution fusion | flops 1107300352 | bytes 34877444 | tf_op jit(solution)/shard_map/while/body/eval_jaxpr/sub | solution.py:85
  135.6 13.6 %fusion.155 = bf16[2,1024,64]{1,2,0:T(8,128)(2,1)S(1)} fusion(bf16[4096,2,64]{0,2,1:T(8,128)(2,1)} %get-tuple-element.170, f32[2,1024,4096]{2,1,0:T(8,128)} %get-tuple-element.141, f32[2,1024]{1,0:T(2,128)S(1)} %get-tuple-element.142), kind=kOutput, calls=%fused_computation.11.clone.1 | convolution fusion | flops 1090650112 | bytes 34873344 | tf_op jit(solution)/shard_map/while/body/eval_jaxpr/hqk,khd->qhd/dot_general | solution.py:87
  149.2 0.2 copy.67
  149.4 0.7 constant_dynamic-update-slice_fusion.2
  150.1 0.6 dynamic_slice.24
  151.4 0.7 iota_compare_fusion.3
  152.0 17.1 %fusion.154 = (f32[2,1024]{1,0:T(2,128)S(1)}, f32[2,1024,4096]{2,1,0:T(8,128)}) fusion(pred[4096]{0:T(1024)(128)(4,1)S(1)} %iota_compare_fusion.3, bf16[4096,2,64]{0,2,1:T(8,128)(2,1)} %get-tuple-element.169, bf16[4096,2,64]{0,2,1:T(8,128)(2,1)} %get-tuple-element.168, s32[]{:T(128)S(6)} %select_n.28), kind=kOutput, calls=%fused_computation.143.clone.1 | convolution fusion | flops 1107300352 | bytes 34877444 | tf_op jit(solution)/shard_map/while/body/eval_jaxpr/sub | solution.py:85
  169.1 13.6 %fusion.155 = bf16[2,1024,64]{1,2,0:T(8,128)(2,1)S(1)} fusion(bf16[4096,2,64]{0,2,1:T(8,128)(2,1)} %get-tuple-element.170, f32[2,1024,4096]{2,1,0:T(8,128)} %get-tuple-element.141, f32[2,1024]{1,0:T(2,128)S(1)} %get-tuple-element.142), kind=kOutput, calls=%fused_computation.11.clone.1 | convolution fusion | flops 1090650112 | bytes 34873344 | tf_op jit(solution)/shard_map/while/body/eval_jaxpr/hqk,khd->qhd/dot_general | solution.py:87
  182.7 0.2 copy.67
  182.9 0.7 constant_dynamic-update-slice_fusion.2
  183.6 0.6 dynamic_slice.24
  184.9 0.7 iota_compare_fusion.3
  185.5 17.1 %fusion.154 = (f32[2,1024]{1,0:T(2,128)S(1)}, f32[2,1024,4096]{2,1,0:T(8,128)}) fusion(pred[4096]{0:T(1024)(128)(4,1)S(1)} %iota_compare_fusion.3, bf16[4096,2,64]{0,2,1:T(8,128)(2,1)} %get-tuple-element.169, bf16[4096,2,64]{0,2,1:T(8,128)(2,1)} %get-tuple-element.168, s32[]{:T(128)S(6)} %select_n.28), kind=kOutput, calls=%fused_computation.143.clone.1 | convolution fusion | flops 1107300352 | bytes 34877444 | tf_op jit(solution)/shard_map/while/body/eval_jaxpr/sub | solution.py:85
  202.6 13.6 %fusion.155 = bf16[2,1024,64]{1,2,0:T(8,128)(2,1)S(1)} fusion(bf16[4096,2,64]{0,2,1:T(8,128)(2,1)} %get-tuple-element.170, f32[2,1024,4096]{2,1,0:T(8,128)} %get-tuple-element.141, f32[2,1024]{1,0:T(2,128)S(1)} %get-tuple-element.142), kind=kOutput, calls=%fused_computation.11.clone.1 | convolution fusion | flops 1090650112 | bytes 34873344 | tf_op jit(solution)/shard_map/while/body/eval_jaxpr/hqk,khd->qhd/dot_general | solution.py:87
  216.2 0.2 copy.67
  216.4 0.7 constant_dynamic-update-slice_fusion.2
  217.1 4.6 %all-to-all-start.2 = ((bf16[8,512,128]{2,1,0:T(8,128)(2,1)}), bf16[8,512,128]{2,1,0:T(8,128)(2,1)S(1)}, u32[]{:S(2)}, u32[]{:S(2)}) async-start(bf16[8,512,128]{2,1,0:T(8,128)(2,1)} %bitcast.57), calls=%async_computation.2 | async-start | bytes 2097152 | tf_op jit(solution)/shard_map/all_to_all | solution.py:135
  222.4 14.3 %all-to-all-done.2 = bf16[8,512,128]{2,1,0:T(8,128)(2,1)S(1)} async-done(((bf16[8,512,128]{2,1,0:T(8,128)(2,1)}), bf16[8,512,128]{2,1,0:T(8,128)(2,1)S(1)}, u32[]{:S(2)}, u32[]{:S(2)}) %all-to-all-start.2) | async-done | bytes 1048608 | tf_op jit(solution)/shard_map/all_to_all | solution.py:135
  236.7 1.3 copy.50
  238.0 2.9 fusion.131
  240.9 1.3 copy-done.1
  242.3 0.3 multiply_reduce_fusion.2
  242.6 0.0 all-gather.2.cloned.1.call-done
  242.7 26.0 %fusion.73.clone.5 = bf16[512,4096]{1,0:T(8,128)(2,1)S(1)} fusion(bf16[1024,8192]{1,0:T(8,128)(2,1)} %all-gather.2.cloned.1.call-done, f32[512,1024]{1,0:T(8,128)} %copy-done.1, f32[1024]{0:T(1024)S(1)} %copy-done.6, f32[1024]{0:T(1024)S(1)} %copy-done.7, f32[512]{0:T(512)S(1)} %add_rsqrt_fusion.1, ...), kind=kOutput, calls=%fused_computation.24.clone.clone.clone.clone.clone.clone.2 | convolution fusion | flops 4433903616 | bytes 14692352 | tf_op jit(solution)/shard_map/dot_general | solution.py:100
  268.7 7.9 %fusion.132 = (f32[512]{0:T(512)S(1)}, f32[512,1024]{1,0:T(8,128)S(1)}) fusion(f32[1024]{0:T(1024)S(1)} %copy-done.6, f32[1024]{0:T(1024)S(1)} %copy-done.7, f32[512]{0:T(512)S(1)} %add_rsqrt_fusion.1, f32[512,1024]{1,0:T(8,128)S(1)} %copy-done.2, f32[512]{0:T(512)S(1)} %broadcast_multiply_fusion.1, bf16[1024,8192]{1,0:T(8,128)(2,1)} %all-gather.2.cloned.1.call-done, ...), kind=kOutput, calls=%fused_computation.147 | convolution fusion | flops 4299161088 | bytes 16791552 | tf_op jit(solution)/shard_map/dot_general | solution.py:105
  276.6 0.3 multiply_reduce_fusion.1
  277.0 1.5 multiply_reduce_fusion
  278.5 0.6 broadcast_in_dim.32
  279.1 4.2 %all-to-all-start.3 = ((f32[8,1,1024]{2,1,0:T(1,128)}), f32[8,1,1024]{2,1,0:T(1,128)S(1)}, u32[]{:S(2)}, u32[]{:S(2)}) async-start(f32[8,1,1024]{2,1,0:T(1,128)} %broadcast_in_dim.32), calls=%async_computation.3 | async-start | bytes 65536 | tf_op jit(solution)/shard_map/all_to_all | solution.py:46
  283.3 0.1 multiply_reduce_fusion.3
  283.5 4.6 %all-to-all-done.3 = f32[8,1,1024]{2,1,0:T(1,128)S(1)} async-done(((f32[8,1,1024]{2,1,0:T(1,128)}), f32[8,1,1024]{2,1,0:T(1,128)S(1)}, u32[]{:S(2)}, u32[]{:S(2)}) %all-to-all-start.3) | async-done | bytes 32800 | tf_op jit(solution)/shard_map/all_to_all | solution.py:46
  288.1 0.6 multiply_reduce_fusion.4
  289.4 0.6 fusion.123
  290.1 0.5 broadcast.121
  290.6 0.8 reduce.1
  291.4 0.6 reshape.80
  292.0 6.7 %all-to-all-start.4 = ((bf16[16,2,512]{2,1,0:T(2,128)(2,1)}), bf16[16,2,512]{2,1,0:T(2,128)(2,1)S(1)}, u32[]{:S(2)}, u32[]{:S(2)}) async-start(bf16[16,2,512]{2,1,0:T(2,128)(2,1)} %reshape.80), calls=%async_computation.4 | async-start | bytes 65536 | tf_op jit(solution)/shard_map/all_to_all | solution.py:46
  298.7 6.4 %all-to-all-done.4 = bf16[16,2,512]{2,1,0:T(2,128)(2,1)S(1)} async-done(((bf16[16,2,512]{2,1,0:T(2,128)(2,1)}), bf16[16,2,512]{2,1,0:T(2,128)(2,1)S(1)}, u32[]{:S(2)}, u32[]{:S(2)}) %all-to-all-start.4) | async-done | bytes 32800 | tf_op jit(solution)/shard_map/all_to_all | solution.py:46
  305.2 0.3 exponential_reduce_fusion
  305.5 0.5 log_subtract_fusion
  (29 shorter events, 0.2 us)
Async XLA Ops:
  7.2 230.8 %copy-start = (bf16[1024,1024]{1,0:T(8,128)(2,1)S(1)}, bf16[1024,1024]{1,0:T(8,128)(2,1)}, u32[]{:S(2)}) copy-start(bf16[1024,1024]{1,0:T(8,128)(2,1)} %param.17) | copy-start | bytes 6291460
  7.2 235.5 %all-gather.2.cloned.1.call-start = ((), (), s32[]{:S(2)}) async-start(), calls=%async_computation.5 | async-start | bytes 17825792 | tf_op jit(solution)/shard_map/all_gather | solution.py:14
  46.5 25.9 %all-to-all-start.1 = ((bf16[8,256,3,128]{3,1,2,0:T(8,128)(2,1)}), bf16[8,256,3,128]{3,1,2,0:T(8,128)(2,1)}, u32[]{:S(2)}, u32[]{:S(2)}) async-start(bf16[8,256,3,128]{3,1,2,0:T(8,128)(2,1)} %get-tuple-element.89), calls=%async_computation.1 | async-start | bytes 3145728 | tf_op jit(solution)/shard_map/all_to_all | solution.py:40
  217.1 25.5 %copy-start.6 = (f32[1024]{0:T(1024)S(1)}, f32[1024]{0:T(1024)}, u32[]{:S(2)}) copy-start(f32[1024]{0:T(1024)} %param.19) | copy-start | bytes 12292
  217.1 25.5 %copy-start.7 = (f32[1024]{0:T(1024)S(1)}, f32[1024]{0:T(1024)}, u32[]{:S(2)}) copy-start(f32[1024]{0:T(1024)} %param.18) | copy-start | bytes 12292
  217.1 19.6 %all-to-all-start.2 = ((bf16[8,512,128]{2,1,0:T(8,128)(2,1)}), bf16[8,512,128]{2,1,0:T(8,128)(2,1)S(1)}, u32[]{:S(2)}, u32[]{:S(2)}) async-start(bf16[8,512,128]{2,1,0:T(8,128)(2,1)} %bitcast.57), calls=%async_computation.2 | async-start | bytes 2097152 | tf_op jit(solution)/shard_map/all_to_all | solution.py:135
  240.9 1.4 copy-start.1
  242.7 26.0 %copy-start.2 = (f32[512,1024]{1,0:T(8,128)S(1)}, f32[512,1024]{1,0:T(8,128)}, u32[]{:S(2)}) copy-start(f32[512,1024]{1,0:T(8,128)} %copy-done.1) | copy-start | bytes 6291460
  268.6 8.3 %copy-start.4 = (f32[1024]{0:T(1024)S(1)}, f32[1024]{0:T(1024)}, u32[]{:S(2)}) copy-start(f32[1024]{0:T(1024)} %param.23) | copy-start | bytes 12292
  268.7 8.3 %copy-start.5 = (f32[1024]{0:T(1024)S(1)}, f32[1024]{0:T(1024)}, u32[]{:S(2)}) copy-start(f32[1024]{0:T(1024)} %param.22) | copy-start | bytes 12292
  268.7 14.7 %copy-start.3 = (f32[8,1024]{1,0:T(8,128)S(1)}, f32[8,1024]{1,0:T(8,128)}, u32[]{:S(2)}) copy-start(f32[8,1024]{1,0:T(8,128)} %param.24) | copy-start | bytes 98308
  268.7 36.5 %copy-start.8 = (s32[8]{0:T(128)S(1)}, s32[8]{0:T(128)}, u32[]{:S(2)}) copy-start(s32[8]{0:T(128)} %param.25) | copy-start | bytes 100
  279.1 9.0 %all-to-all-start.3 = ((f32[8,1,1024]{2,1,0:T(1,128)}), f32[8,1,1024]{2,1,0:T(1,128)S(1)}, u32[]{:S(2)}, u32[]{:S(2)}) async-start(f32[8,1,1024]{2,1,0:T(1,128)} %broadcast_in_dim.32), calls=%async_computation.3 | async-start | bytes 65536 | tf_op jit(solution)/shard_map/all_to_all | solution.py:46
  292.0 13.1 %all-to-all-start.4 = ((bf16[16,2,512]{2,1,0:T(2,128)(2,1)}), bf16[16,2,512]{2,1,0:T(2,128)(2,1)S(1)}, u32[]{:S(2)}, u32[]{:S(2)}) async-start(bf16[16,2,512]{2,1,0:T(2,128)(2,1)} %reshape.80), calls=%async_computation.4 | async-start | bytes 65536 | tf_op jit(solution)/shard_map/all_to_all | solution.py:46
Sparse Core Ops, SparseCore 0:
  10.1 114.0 all-gather.1
where the time goes:
time: 314 us; the launch traced here: 313 us
  matrix products  167 us (53%)
  waiting for transfers between devices  46.1 us (15%)
  blocking collectives  27.2 us (9%)
  local copies, waits for them, and re-layouts  21.2 us (7%)
  starting transfers between devices  20.7 us (7%)
  between operations  15.6 us (5%)
  other arithmetic  12.1 us (4%)
    sub x4, matrix products, one_block(): expo = jnp.exp(scores - highest)  68.8 us
    dot_general x4, matrix products, one_block(): jnp.einsum('hqk,khd->qhd', probs, value_all, preferred_element_type=jnp.f...  54.7 us
    all_to_all x1, blocking collectives, several_exchanges(): lax.all_to_all(slab, axis, split_axis=0, concat_axis=0, tiled=True)  27.2 us
    dot_general x1, matrix products, expand_inner(): jnp.dot(rows_in, up_full, preferred_element_type=jnp.float32)  26 us
    all_to_all x1, waiting for transfers between devices, several_exchanges(): lax.all_to_all(slab, axis, split_axis=0, concat_axis=0, tiled=True)  20.7 us
    all_to_all x1, waiting for transfers between devices, body(): lax.all_to_all(attended, 'seq', split_axis=0, concat_axis=1, tiled=True)  14.3 us
    all_to_all x2, waiting for transfers between devices, sent_to_all(): return lax.all_to_all(copies, axis, split_axis=0, concat_axis=0, tiled=True)  11.1 us
    all_to_all x2, starting transfers between devices, sent_to_all(): return lax.all_to_all(copies, axis, split_axis=0, concat_axis=0, tiled=True)  10.9 us
  transfers between devices with their start and end apart: 5, of which 4 were waited for; matrix products, arithmetic and copies ran while one was open for 50% of the time, Pallas kernels for 0%

commit v1 on v0

v1 whole, which is shorter than its diff:
```python
import math
import functools

import jax
import jax.numpy as jnp
from jax import lax
from jax.experimental import pallas as pl
from jax.experimental.pallas import tpu as pltpu
from jax.sharding import PartitionSpec as P

MESH = pl.DeviceIdType.MESH
BF = jnp.bfloat16
F32 = jnp.float32
NEG = -1e30
KB = 1024
QT = 512
NT = 1024 // QT
TILES = 8 * NT
U = 4
ITERS = TILES // U
SCALE = math.log2(math.e) / 8.0


def attend_kernel(
    len_ref, x_ref, w_ref, up_ref, dn_ref, att_ref, wf_ref,
    xbuf, wqkv, kscr, vscr, qscr, acc, mx, s_a, s_b, al, stage, wv,
    lsem, hs, hr, ds, dr, ws, wr, ps, pr, osem,
):
    s = lax.axis_index("seq")
    g = lax.axis_index("grp")
    c = lax.rem(s, 2)
    z = s // 2
    gx = lax.rem(g, 4)
    gy = g // 4
    mate = {"seq": s + 1 - 2 * c}
    zup = {"seq": lax.rem(s + 2, 8)}
    zdn = {"seq": lax.rem(s + 6, 8)}

    def wrap(v):
        return lax.rem(v, 4)

    def peer(axis, step):
        if axis == 0:
            return {"grp": gy * 4 + wrap(gx + step)}
        return {"grp": wrap(gy + step) * 4 + gx}

    loads = [pltpu.make_async_copy(x_ref, xbuf.at[0, pl.ds(0, 512)], lsem.at[0])]
    for t in range(3):
        cols = pl.ds(pl.multiple_of(t * 1024 + c * 512, 512), 512)
        loads.append(
            pltpu.make_async_copy(w_ref.at[:, cols], wqkv.at[:, pl.ds(t * 512, 512)], lsem.at[1 + t])
        )
    loads.append(pltpu.make_async_copy(up_ref, wv.at[0], lsem.at[4]))
    loads.append(pltpu.make_async_copy(dn_ref, wv.at[1], lsem.at[5]))
    for cp in loads:
        cp.start()

    peers = [mate, zup, zdn, peer(0, 1), peer(0, 3), peer(1, 1), peer(1, 3)]
    barrier = pltpu.get_barrier_semaphore()
    for d in peers:
        pl.semaphore_signal(barrier, inc=1, device_id=d, device_id_type=MESH)
    pl.semaphore_wait(barrier, len(peers))

    def rcopy(src, dst, ssem, rsem, dev):
        return pltpu.make_async_remote_copy(
            src_ref=src, dst_ref=dst, send_sem=ssem, recv_sem=rsem, device_id=dev, device_id_type=MESH
        )

    def h_piece(p):
        return xbuf.at[0, pl.ds(p * 256, 256)]

    def x_quarter(j, q):
        return xbuf.at[j, pl.ds(q * 256, 256)]

    h_own = rcopy(xbuf.at[0, pl.ds(0, 512)], xbuf.at[0, pl.ds(512, 512)], ds.at[0], dr.at[0], mate)
    h_dn = [rcopy(h_piece(p), x_quarter(1 + p, 0), hs.at[p], hr.at[p], zdn) for p in range(2)]
    h_up = [rcopy(h_piece(p), x_quarter(1 + p, 2), hs.at[2 + p], hr.at[2 + p], zup) for p in range(2)]
    f_dn = rcopy(x_quarter(1, 0), x_quarter(3, 0), hs.at[4], hr.at[4], zdn)
    f_up = rcopy(x_quarter(2, 2), x_quarter(3, 1), hs.at[5], hr.at[5], zup)
    h_mate = []
    for k, (j, a, b) in enumerate([(1, 0, 1), (1, 2, 3), (2, 0, 1), (2, 2, 3), (3, 0, 2), (3, 1, 3)]):
        h_mate.append(rcopy(x_quarter(j, a), x_quarter(j, b), ds.at[1 + k], dr.at[1 + k], mate))

    def origin_row(t, d1, d2):
        dx, dy = (d1, d2) if t == 0 else (d2, d1)
        return (wrap(gy + dy) * 4 + wrap(gx + dx)) * 64 + t * 32

    def w_reg(t, d1, d2, lo, n):
        return wf_ref.at[c, pl.ds(pl.multiple_of(origin_row(t, d1, d2) + lo, 16), n), :]

    w1, w2, w3, w4 = {}, {}, {}, {}
    for t in range(2):
        mine = wv.at[c, pl.ds(t * 32, 32), :]
        a1, a2 = t, 1 - t
        for i, (step, seen) in enumerate([(1, 3), (3, 1)]):
            w1[t, i] = rcopy(mine, w_reg(t, 0, 0, 0, 32), ws.at[t, i], wr.at[t, seen, 0, 0], peer(a1, step))
            w2[t, i] = rcopy(
                w_reg(t, seen, 0, 16 * i, 16), w_reg(t, seen, 0, 16 * i, 16),
                ws.at[t, 2 + i], wr.at[t, 2, 0, i], peer(a1, step),
            )
            for d1 in range(4):
                src = mine if d1 == 0 else w_reg(t, d1, 0, 0, 32)
                w3[t, d1, i] = rcopy(
                    src, w_reg(t, d1, 0, 0, 32), ws.at[t, 4 + 2 * d1 + i], wr.at[t, d1, seen, 0], peer(a2, step)
                )
                w4[t, d1, i] = rcopy(
                    w_reg(t, d1, seen, 16 * i, 16), w_reg(t, d1, seen, 16 * i, 16),
                    ws.at[t, 12 + 2 * d1 + i], wr.at[t, d1, 2, i], peer(a2, step),
                )
    w5 = {}
    for t in range(2):
        for d1 in range(4):
            for d2 in range(4):
                if d1 or d2:
                    w5[t, d1, d2] = rcopy(
                        w_reg(t, d1, d2, 0, 32), w_reg(t, d1, d2, 0, 32),
                        ps.at[t, d1, d2], pr.at[t, d1, d2], mate,
                    )

    def w_arrived(t, d1, d2, k, n):
        reg = w_reg(t, d1, d2, 16 * k, n)
        pltpu.make_async_copy(reg, reg, wr.at[t, d1, d2, k]).wait()

    loads[0].wait()
    for cp in h_dn + h_up + [h_own]:
        cp.start()
    loads[4].wait()
    loads[5].wait()
    for t in range(2):
        for i in range(2):
            w1[t, i].start()
    for t in range(2):
        for i in range(2):
            w3[t, 0, i].start()
    own_rows = pl.ds(pl.multiple_of(g * 64, 64), 64)
    outs = [pltpu.make_async_copy(wv.at[k], wf_ref.at[k, own_rows, :], lsem.at[6 + k]) for k in range(2)]
    for cp in outs:
        cp.start()

    qscr[...] = jnp.zeros_like(qscr)
    for h in range(8):
        qscr[h, 128:144, :] = (lax.broadcasted_iota(jnp.int32, (16, KB), 0) == 0).astype(BF)
        vscr[h, 64:80, :] = jnp.ones((16, KB), BF)
    acc[...] = jnp.zeros_like(acc)
    mx[...] = jnp.full_like(mx, NEG)
    length = len_ref[0]

    for k in range(3):
        loads[1 + k].wait()
    h_own.wait_recv()
    for i in range(2):
        q = jnp.dot(xbuf[0], wqkv[:, 256 * i : 256 * i + 256], preferred_element_type=F32)
        qt = (q * SCALE).T.astype(BF)
        for u in range(4):
            h = 4 * i + u
            qscr[h, (u % 2) * 64 : (u % 2) * 64 + 64, :] = qt[64 * u : 64 * u + 64]

    bufs = [s_a, s_b]

    def scores(h, t, sref, slot):
        sl = pl.ds(pl.multiple_of(t * QT, QT), QT)
        sc = jnp.dot(kscr[h // 2], qscr[h, :, sl], preferred_element_type=F32)
        sref[...] = sc
        old = mx[h, :, sl]
        new = jnp.maximum(old, jnp.max(sc, axis=0, keepdims=True))
        mx[h, :, sl] = new
        al[slot] = jnp.exp2(old - new)
        al[slot + 2] = new

    def values(h, t, sref, slot):
        sl = pl.ds(pl.multiple_of(t * QT, QT), QT)
        p = jnp.exp2(sref[...] - al[slot + 2]).astype(BF)
        acc[h, :, sl] = acc[h, :, sl] * al[slot] + jnp.dot(vscr[h], p, preferred_element_type=F32)

    def events(e):
        def at(k, fn):
            @pl.when(e == k)
            def _():
                fn()

        def hidden_next(j):
            if j == 1:
                h_dn[0].wait_recv()
                h_up[0].wait_recv()
                f_dn.start()
                h_mate[0].start()
                h_mate[1].start()
            elif j == 2:
                h_dn[1].wait_recv()
                h_up[1].wait_recv()
                f_up.start()
                h_mate[2].start()
                h_mate[3].start()
            else:
                f_dn.wait_recv()
                f_up.wait_recv()
                h_mate[4].start()
                h_mate[5].start()

        def w_step2():
            for t in range(2):
                w_arrived(t, 3, 0, 0, 32)
                w_arrived(t, 1, 0, 0, 32)
                for i in range(2):
                    w2[t, i].start()
                for d1 in (1, 3):
                    for i in range(2):
                        w3[t, d1, i].start()

        def w_step3():
            for t in range(2):
                w_arrived(t, 2, 0, 0, 16)
                w_arrived(t, 2, 0, 1, 16)
                w_arrived(t, 0, 1, 0, 32)
                w_arrived(t, 0, 3, 0, 32)
                for i in range(2):
                    w3[t, 2, i].start()
                for i in range(2):
                    w4[t, 0, i].start()
                for d in ((1, 0), (2, 0), (3, 0), (0, 1), (0, 3)):
                    w5[t, d[0], d[1]].start()

        def w_step4():
            for t in range(2):
                for d1 in (1, 3):
                    w_arrived(t, d1, 1, 0, 32)
                    w_arrived(t, d1, 3, 0, 32)
                    for i in range(2):
                        w4[t, d1, i].start()
                    w5[t, d1, 1].start()
                    w5[t, d1, 3].start()

        def w_step5():
            for t in range(2):
                w_arrived(t, 2, 1, 0, 32)
                w_arrived(t, 2, 3, 0, 32)
                for i in range(2):
                    w4[t, 2, i].start()
                w5[t, 2, 1].start()
                w5[t, 2, 3].start()
                w_arrived(t, 0, 2, 0, 16)
                w_arrived(t, 0, 2, 1, 16)
                w5[t, 0, 2].start()

        def w_step6():
            for t in range(2):
                for d1 in (1, 3, 2):
                    w_arrived(t, d1, 2, 0, 16)
                    w_arrived(t, d1, 2, 1, 16)
                    w5[t, d1, 2].start()

        at(2, w_step2)
        at(3, lambda: hidden_next(1))
        at(5, w_step3)
        at(7, lambda: hidden_next(2))
        at(9, w_step4)
        at(11, lambda: hidden_next(3))
        at(12, w_step5)
        at(15, w_step6)

    def chunk(j, carry):
        for k in range(1, 4):

            @pl.when(j == k)
            def _():
                h_mate[2 * k - 2].wait_recv()
                h_mate[2 * k - 1].wait_recv()

        edge = jnp.logical_or(j == 0, j == 3).astype(jnp.int32)
        for q in range(4):
            dz = edge * jnp.where(j == 0, 0, 2) + (1 - edge) * (1 if q < 2 else 3)
            cc = edge * (q // 2) + (1 - edge) * (q % 2)
            pp = edge * (q % 2) + (1 - edge) * (j - 1)
            base = (wrap(z + dz) * 2 + c + cc - 2 * c * cc) * 512 + pp * 256
            pos = lax.broadcasted_iota(jnp.int32, (256, 128), 0) + base
            bias = jnp.where(pos < length, 0.0, NEG).astype(BF)
            for pr_ in range(4):
                kscr[pr_, q * 256 : q * 256 + 256, 128:256] = bias
        xj = xbuf[j]
        for i in range(2):
            kk = jnp.dot(xj, wqkv[:, 512 + 256 * i : 768 + 256 * i], preferred_element_type=F32).astype(BF)
            kscr[2 * i, :, 0:128] = kk[:, 0:128]
            kscr[2 * i + 1, :, 0:128] = kk[:, 128:256]
            vt = jnp.dot(xj, wqkv[:, 1024 + 256 * i : 1280 + 256 * i], preferred_element_type=F32).T.astype(BF)
            for u in range(4):
                vscr[4 * i + u, 0:64, :] = vt[64 * u : 64 * u + 64]

        scores(0, 0, s_a, 0)

        def it(k, carry2):
            events(j * ITERS + k)
            for u in range(U):
                i = k * U + u
                nx = jnp.minimum(i + 1, TILES - 1)
                scores(nx // NT, lax.rem(nx, NT), bufs[(u + 1) % 2], (u + 1) % 2)
                values(i // NT, i % NT, bufs[u % 2], u % 2)
            return carry2

        lax.fori_loop(0, ITERS, it, 0)
        return carry

    lax.fori_loop(0, 4, chunk, 0)

    for pr_ in range(4):
        pair = []
        for h in (2 * pr_, 2 * pr_ + 1):
            pair.append(acc[h, 0:64, :] / acc[h, 64:65, :])
        both = jnp.concatenate(pair, axis=0)
        stage[:, 128 * pr_ : 128 * pr_ + 128] = both.T.astype(BF)
    my_cols = pl.ds(pl.multiple_of(c * 512, 512), 512)
    o_mate = rcopy(stage.at[pl.ds(512, 512)], att_ref.at[:, my_cols], osem.at[0], osem.at[1], mate)
    o_mine = pltpu.make_async_copy(stage.at[pl.ds(0, 512)], att_ref.at[:, my_cols], osem.at[2])
    o_mate.start()
    o_mine.start()
    for cp in w5.values():
        cp.wait()
    for group in (w1, w2, w3, w4):
        for cp in group.values():
            cp.wait_send()
    for cp in outs:
        cp.wait()
    for cp in h_dn + h_up + [f_dn, f_up, h_own] + h_mate:
        cp.wait_send()
    o_mine.wait()
    o_mate.wait()


def attend(length, tokens, project, up, down):
    any_spec = pl.BlockSpec(memory_space=pl.ANY)
    dma = pltpu.SemaphoreType.DMA
    return pl.pallas_call(
        attend_kernel,
        name="attend",
        out_shape=(
            jax.ShapeDtypeStruct((512, 1024), BF),
            jax.ShapeDtypeStruct((2, 1024, 4096), BF),
        ),
        in_specs=[pl.BlockSpec(memory_space=pltpu.SMEM)] + [any_spec] * 4,
        out_specs=(any_spec, any_spec),
        scratch_shapes=[
            pltpu.VMEM((4, 1024, 1024), BF),
            pltpu.VMEM((1024, 1536), BF),
            pltpu.VMEM((4, KB, 256), BF),
            pltpu.VMEM((8, 80, KB), BF),
            pltpu.VMEM((8, 256, 1024), BF),
            pltpu.VMEM((8, 80, 1024), F32),
            pltpu.VMEM((8, 1, 1024), F32),
            pltpu.VMEM((KB, QT), F32),
            pltpu.VMEM((KB, QT), F32),
            pltpu.VMEM((4, 1, QT), F32),
            pltpu.VMEM((1024, 512), BF),
            pltpu.VMEM((2, 64, 4096), BF),
            dma((8,)), dma((6,)), dma((6,)), dma((7,)), dma((7,)),
            dma((2, 20)), dma((2, 4, 4, 2)), dma((2, 4, 4)), dma((2, 4, 4)), dma((3,)),
        ],
        compiler_params=pltpu.CompilerParams(
            collective_id=0, has_side_effects=True, vmem_limit_bytes=62 * 2**20
        ),
    )(length, tokens, project, up, down)


def layer_norm(values, gain, shift):
    average = jnp.mean(values, axis=-1, keepdims=True)
    centred = values - average
    variance = jnp.mean(centred * centred, axis=-1, keepdims=True)
    return centred * lax.rsqrt(variance + 1e-05) * gain + shift


FC = 512
RB = 256


def feed_kernel(info_ref, att_ref, tok_ref, wo_ref, vec_ref, up_ref, dn_ref, out_ref, tot_ref, normed, acc):
    i = pl.program_id(0)

    @pl.when(i == 0)
    def _():
        for r in range(512 // RB):
            rows = pl.ds(r * RB, RB)
            mixed = jnp.dot(att_ref[rows, :], wo_ref[...], preferred_element_type=F32)
            mixed = mixed + tok_ref[rows, :].astype(F32)
            n = layer_norm(mixed, vec_ref[0:1, :], vec_ref[1:2, :]).astype(BF)
            normed[rows, :] = n
            acc[rows, :] = n.astype(F32)

    for r in range(512 // RB):
        rows = pl.ds(r * RB, RB)
        h = jnp.dot(normed[rows, :], up_ref[0], preferred_element_type=F32)
        inner = (0.5 * h * (1.0 + lax.erf(h * math.sqrt(0.5)))).astype(BF)
        acc[rows, :] += lax.dot_general(
            inner, dn_ref[0], (((1,), (1,)), ((), ())), preferred_element_type=F32
        )

    @pl.when(i == 4096 // FC - 1)
    def _():
        total = jnp.zeros((1, 1024), F32)
        for r in range(512 // RB):
            rows = pl.ds(r * RB, RB)
            final = layer_norm(acc[rows, :], vec_ref[2:3, :], vec_ref[3:4, :])
            out_ref[rows, :] = final.astype(BF)
            pos = lax.broadcasted_iota(jnp.int32, (RB, 1), 0) + (info_ref[1] + r * RB)
            valid = (pos < info_ref[0]).astype(F32)
            total = total + jnp.sum(final * valid, axis=0, keepdims=True)
        tot_ref[...] = total


def feed(info, att, tokens, output_weight, vecs, wf):
    whole = lambda shape: pl.BlockSpec(shape, lambda i: (0,) * len(shape))
    return pl.pallas_call(
        feed_kernel,
        name="feed",
        grid=(4096 // FC,),
        out_shape=(jax.ShapeDtypeStruct((512, 1024), BF), jax.ShapeDtypeStruct((1, 1024), F32)),
        in_specs=[
            pl.BlockSpec(memory_space=pltpu.SMEM),
            whole((512, 1024)),
            whole((512, 1024)),
            whole((1024, 1024)),
            whole((4, 1024)),
            pl.BlockSpec((1, 1024, FC), lambda i: (0, 0, i)),
            pl.BlockSpec((1, 1024, FC), lambda i: (1, 0, i)),
        ],
        out_specs=(whole((512, 1024)), whole((1, 1024))),
        scratch_shapes=[pltpu.VMEM((512, 1024), BF), pltpu.VMEM((512, 1024), F32)],
        compiler_params=pltpu.CompilerParams(
            dimension_semantics=("arbitrary",), vmem_limit_bytes=56 * 2**20
        ),
    )(info, att, tokens, output_weight, vecs, wf, wf)


def loss_kernel(len_ref, pos_ref, tot_ref, q_ref, emb_ref, loss_ref, parts, sent, passages, ssem, rsem, ssem2, rsem2):
    s = lax.axis_index("seq")
    g = lax.axis_index("grp")
    barrier = pltpu.get_barrier_semaphore()
    for d in range(1, 8):
        pl.semaphore_signal(barrier, inc=1, device_id={"seq": lax.rem(s + d, 8)}, device_id_type=MESH)
    for d in range(1, 16):
        pl.semaphore_signal(barrier, inc=1, device_id={"grp": lax.rem(g + d, 16)}, device_id_type=MESH)
    pl.semaphore_wait(barrier, 22)
    first = []
    for d in range(1, 8):
        cp = pltpu.make_async_remote_copy(
            src_ref=tot_ref, dst_ref=parts.at[d], send_sem=ssem.at[d], recv_sem=rsem.at[d],
            device_id={"seq": lax.rem(s + d, 8)}, device_id_type=MESH,
        )
        cp.start()
        first.append(cp)
    qv = q_ref[...]
    short_q = (qv / jnp.sqrt(jnp.sum(qv * qv, axis=-1, keepdims=True) + 1e-06)).astype(BF)
    for cp in first:
        cp.wait_recv()
    total = tot_ref[...]
    for d in range(1, 8):
        total = total + parts[d]
    pooled = total / len_ref[0].astype(F32)
    emb = pooled / jnp.sqrt(jnp.sum(pooled * pooled, axis=-1, keepdims=True) + 1e-06)
    emb_ref[...] = emb
    sent[...] = emb
    second = []
    for d in range(1, 16):
        cp = pltpu.make_async_remote_copy(
            src_ref=sent, dst_ref=passages.at[d], send_sem=ssem2.at[d], recv_sem=rsem2.at[d],
            device_id={"grp": lax.rem(g + d, 16)}, device_id_type=MESH,
        )
        cp.start()
        second.append(cp)
    for cp in second:
        cp.wait_recv()
    rows = [emb] + [passages[d] for d in range(1, 16)]
    allp = jnp.concatenate(rows, axis=0).astype(BF)
    logits = 20.0 * lax.dot_general(
        short_q, allp, (((1,), (1,)), ((), ())), preferred_element_type=F32
    )
    ids = lax.rem(g + 16 - lax.broadcasted_iota(jnp.int32, (8, 16), 1), 16)
    picked = jnp.sum(jnp.where(pos_ref[...] == ids, logits, 0.0), axis=1, keepdims=True)
    loss_ref[...] = jnp.log(jnp.sum(jnp.exp(logits), axis=1, keepdims=True)) - picked
    for cp in first + second:
        cp.wait_send()


def losses(length, positive, total, queries):
    vm = pl.BlockSpec(memory_space=pltpu.VMEM)
    dma = pltpu.SemaphoreType.DMA
    return pl.pallas_call(
        loss_kernel,
        name="losses",
        out_shape=(jax.ShapeDtypeStruct((1, 1024), F32), jax.ShapeDtypeStruct((8, 1), F32)),
        in_specs=[pl.BlockSpec(memory_space=pltpu.SMEM), vm, vm, vm],
        out_specs=(vm, vm),
        scratch_shapes=[
            pltpu.VMEM((8, 1, 1024), F32),
            pltpu.VMEM((1, 1024), F32),
            pltpu.VMEM((16, 1, 1024), F32),
            dma((8,)), dma((8,)), dma((16,)), dma((16,)),
        ],
        compiler_params=pltpu.CompilerParams(collective_id=1, has_side_effects=True),
    )(length, positive, total, queries)


def body(
    hidden_in, lengths, project_weight, output_weight, first_gain, first_shift,
    up_weight, down_weight, second_gain, second_shift, queries, positive,
):
    tokens = hidden_in[0]
    att, wf = attend(lengths, tokens, project_weight, up_weight, down_weight)
    vecs = jnp.stack([first_gain, first_shift, second_gain, second_shift])
    info = jnp.concatenate([lengths, (lax.axis_index("seq") * 512)[None].astype(jnp.int32)])
    final, total = feed(info, att, tokens, output_weight, vecs, wf)
    embedding, loss = losses(lengths, positive[:, None], total, queries)
    return final[None], embedding, loss[:, 0]


def solution(mesh):
    in_specs = (
        P("grp", "seq", None), P("grp"), P(), P(), P(), P(),
        P("grp", None), P("grp", None), P(), P(), P("grp", None), P("grp"),
    )
    out_specs = (P("grp", "seq", None), P("grp", None), P("grp"))
    return jax.shard_map(body, mesh=mesh, in_specs=in_specs, out_specs=out_specs, check_vma=False)
```

time: 314 us -> 113 us (0.36)
  matrix products: 167 us -> 0 us
  Pallas kernels: 0 us -> 106 us
  waiting for transfers between devices: 46.1 us -> 0 us
  blocking collectives: 27.2 us -> 0 us
  starting transfers between devices: 20.7 us -> 0 us
  local copies, waits for them, and re-layouts: 21.2 us -> 1.97 us
  between operations: 15.6 us -> 1.37 us
  other arithmetic: 12.1 us -> 2.57 us
    pallas_call x0 -> x3, Pallas kernels: none -> 106 us  [the longest x1 75.8 us: attend(): pl.pallas_call(attend_kernel, name='attend', out_shape=(jax.ShapeDtypeStr...]
    dot_general x9 -> x0, matrix products: 98.4 us -> none  [the longest x4 54.7 us: one_block(): jnp.einsum('hqk,khd->qhd', probs, value_all, preferred_element_type=jnp.f...]
    sub x4 -> x0, matrix products: 68.8 us -> none  [one_block(): expo = jnp.exp(scores - highest)]
    all_to_all x4 -> x0, waiting for transfers between devices: 46.1 us -> none  [the longest x1 20.7 us: several_exchanges(): lax.all_to_all(slab, axis, split_axis=0, concat_axis=0, tiled=True)]
    all_to_all x1 -> x0, blocking collectives: 27.2 us -> none  [several_exchanges(): lax.all_to_all(slab, axis, split_axis=0, concat_axis=0, tiled=True)]
    all_to_all x4 -> x0, starting transfers between devices: 20.6 us -> none  [the longest x2 10.9 us: sent_to_all(): return lax.all_to_all(copies, axis, split_axis=0, concat_axis=0, tiled=True)]
    slice x4 -> x0, local copies, waits for them, and re-layouts: 7.47 us -> none  [the longest x2 2.91 us: attend_local(): value_all = gathered[:, 2, :].reshape(seq_len, head_count, HEAD_DIM)]
    concatenate x2 -> x1, other arithmetic: 4.57 us -> 0.65 us  [body(): jnp.concatenate([lengths, (lax.axis_index('seq') * 512)[None].astype(jnp....]
  transfers between devices with their start and end apart: 5 -> 0, of which waited for: 4 -> 0; matrix products, arithmetic and copies ran while one was open for 50% -> 0% of each run, Pallas kernels for 0% -> 0%
where the time goes in v1:
time: 113 us; the launch traced here: 112 us
  Pallas kernels  106 us (94%)
  other arithmetic  2.57 us (2%)
  local copies, waits for them, and re-layouts  1.97 us (2%)
  between operations  1.37 us (1%)
    pallas_call x1, Pallas kernels, attend(): pl.pallas_call(attend_kernel, name='attend', out_shape=(jax.ShapeDtypeStr...  75.8 us
    pallas_call x1, Pallas kernels, feed(): pl.pallas_call(feed_kernel, name='feed', grid=(4096 // FC,), out_shape=(j...  18.7 us
    pallas_call x1, Pallas kernels, losses(): pl.pallas_call(loss_kernel, name='losses', out_shape=(jax.ShapeDtypeStruc...  11.6 us

profile of v1, /device:TPU:1, one launch (start us, length us, event | category | flops | bytes accessed | tf_op | source)
XLA Modules:
  0.0 112.1 jit_solution(3154536627974118691)
XLA Ops:
  0.6 0.0 copy-start.3
  0.6 0.0 copy-start.2
  0.7 0.0 copy-start.1
  0.7 0.0 copy-start
  1.3 75.8 %attend.1 = (bf16[512,1024]{1,0:T(8,128)(2,1)}, bf16[2,1024,4096]{2,1,0:T(8,128)(2,1)}) custom-call(s32[1]{0:T(128)S(6)} %copy.18.len_ref, bf16[512,1024]{1,0:T(8,128)(2,1)} %bitcast.8, bf16[1024,3072]{1,0:T(8,128)(2,1)} %w_ref.1, bf16[64,4096]{1,0:T(8,128)(2,1)} %up_ref.1, bf16[64,4096]{1,0:T(8,128)(2,1)} %dn_ref.1), custom_call_target="tpu_custom_call" | custom-call | tf_op jit(solution)/shard_map/attend/pallas_call | solution.py:331
  77.2 0.7 pad_add_fusion.info_ref
  77.9 0.0 copy-done.3
  77.9 0.0 copy-done.2
  77.9 0.0 copy-done.1
  77.9 0.0 copy-done
  77.9 0.6 pad_maximum_fusion.vec_ref
  78.5 0.0 copy-start.4
  78.5 18.7 %feed.1 = (bf16[512,1024]{1,0:T(8,128)(2,1)}, f32[1,1024]{1,0:T(1,128)}) custom-call(s32[2]{0:T(128)} %pad_add_fusion.info_ref, bf16[512,1024]{1,0:T(8,128)(2,1)} %get-tuple-element.9.att_ref, bf16[512,1024]{1,0:T(8,128)(2,1)} %bitcast.9, bf16[1024,1024]{1,0:T(8,128)(2,1)} %wo_ref.1, f32[4,1024]{1,0:T(4,128)} %pad_maximum_fusion.vec_ref, ...), custom_call_target="tpu_custom_call" | custom-call | tf_op jit(solution)/shard_map/feed/pallas_call | solution.py:409
  97.2 0.0 copy-done.4
  97.2 0.7 copy.16.pos_ref
  97.9 11.6 %losses.1 = (f32[1,1024]{1,0:T(1,128)}, f32[8,1]{1,0:T(8,128)}) custom-call(s32[1]{0:T(128)S(6)} %copy.18.len_ref, s32[8,1]{1,0:T(8,128)} %copy.16.pos_ref, f32[1,1024]{1,0:T(1,128)} %get-tuple-element.12.tot_ref, f32[8,1024]{1,0:T(8,128)} %q_ref.1), custom_call_target="tpu_custom_call" | custom-call | tf_op jit(solution)/shard_map/losses/pallas_call | solution.py:484
  109.5 1.3 %reduce = f32[8]{0:T(128)} reduce(f32[8,1]{1,0:T(8,128)} %get-tuple-element.14, f32[]{:T(128)} %constant.12), dimensions={1}, to_apply=%get-tuple-element.14.reduce_sub_computation | reduce | bytes 68 | tf_op jit(solution)/shard_map/losses/pallas_call | solution.py:484
  110.8 1.3 %copy.19 = f32[1,1024]{1,0:T(1,128)} copy(f32[1,1024]{1,0:T(1,128)} %get-tuple-element.19) | data formatting | bytes 8192
Async XLA Ops:
  0.6 77.2 %copy-start.3 = (f32[1024]{0:T(1024)S(1)}, f32[1024]{0:T(1024)}, u32[]{:S(2)}) copy-start(f32[1024]{0:T(1024)} %param.16) | copy-start | bytes 12292
  0.6 77.2 %copy-start.2 = (f32[1024]{0:T(1024)S(1)}, f32[1024]{0:T(1024)}, u32[]{:S(2)}) copy-start(f32[1024]{0:T(1024)} %param.17) | copy-start | bytes 12292
  0.7 77.2 %copy-start.1 = (f32[1024]{0:T(1024)S(1)}, f32[1024]{0:T(1024)}, u32[]{:S(2)}) copy-start(f32[1024]{0:T(1024)} %param.20) | copy-start | bytes 12292
  0.7 77.2 %copy-start = (f32[1024]{0:T(1024)S(1)}, f32[1024]{0:T(1024)}, u32[]{:S(2)}) copy-start(f32[1024]{0:T(1024)} %param.21) | copy-start | bytes 12292
  78.5 18.7 %copy-start.4 = (s32[8]{0:T(128)S(1)}, s32[8]{0:T(128)}, u32[]{:S(2)}) copy-start(s32[8]{0:T(128)} %param.23) | copy-start | bytes 100

commit v2 on v1

--- a/solution.py
+++ b/solution.py
@@ -197,66 +197,85 @@
                 h_mate[4].start()
                 h_mate[5].start()
 
-        def w_step2():
+        def arrived(*blocks):
             for t in range(2):
-                w_arrived(t, 3, 0, 0, 32)
-                w_arrived(t, 1, 0, 0, 32)
+                for d1, d2 in blocks:
+                    if d1 == 2 and d2 == 0 or d2 == 2:
+                        w_arrived(t, d1, d2, 0, 16)
+                        w_arrived(t, d1, d2, 1, 16)
+                    else:
+                        w_arrived(t, d1, d2, 0, 32)
+
+        def send(group, *d1s):
+            for t in range(2):
                 for i in range(2):
-                    w2[t, i].start()
-                for d1 in (1, 3):
-                    for i in range(2):
-                        w3[t, d1, i].start()
-
-        def w_step3():
+                    if d1s:
+                        for d1 in d1s:
+                            group[t, d1, i].start()
+                    else:
+                        group[t, i].start()
+
+        def share(*blocks):
             for t in range(2):
-                w_arrived(t, 2, 0, 0, 16)
-                w_arrived(t, 2, 0, 1, 16)
-                w_arrived(t, 0, 1, 0, 32)
-                w_arrived(t, 0, 3, 0, 32)
-                for i in range(2):
-                    w3[t, 2, i].start()
-                for i in range(2):
-                    w4[t, 0, i].start()
-                for d in ((1, 0), (2, 0), (3, 0), (0, 1), (0, 3)):
-                    w5[t, d[0], d[1]].start()
-
-        def w_step4():
-            for t in range(2):
-                for d1 in (1, 3):
-                    w_arrived(t, d1, 1, 0, 32)
-                    w_arrived(t, d1, 3, 0, 32)
-                    for i in range(2):
-                        w4[t, d1, i].start()
-                    w5[t, d1, 1].start()
-                    w5[t, d1, 3].start()
-
-        def w_step5():
-            for t in range(2):
-                w_arrived(t, 2, 1, 0, 32)
-                w_arrived(t, 2, 3, 0, 32)
-                for i in range(2):
-                    w4[t, 2, i].start()
-                w5[t, 2, 1].start()
-                w5[t, 2, 3].start()
-                w_arrived(t, 0, 2, 0, 16)
-                w_arrived(t, 0, 2, 1, 16)
-                w5[t, 0, 2].start()
-
-        def w_step6():
-            for t in range(2):
-                for d1 in (1, 3, 2):
-                    w_arrived(t, d1, 2, 0, 16)
-                    w_arrived(t, d1, 2, 1, 16)
-                    w5[t, d1, 2].start()
-
-        at(2, w_step2)
-        at(3, lambda: hidden_next(1))
-        at(5, w_step3)
+                for d1, d2 in blocks:
+                    w5[t, d1, d2].start()
+
+        def e1():
+            arrived((1, 0), (3, 0))
+            send(w2)
+
+        def e3():
+            hidden_next(1)
+            share((1, 0), (3, 0))
+
+        def e5():
+            arrived((0, 1), (0, 3))
+            send(w4, 0)
+            share((0, 1), (0, 3))
+
+        def e6():
+            arrived((2, 0))
+            send(w3, 2)
+            share((2, 0))
+
+        def e8():
+            arrived((1, 1), (1, 3))
+            send(w4, 1)
+            share((1, 1), (1, 3))
+
+        def e9():
+            arrived((3, 1), (3, 3))
+            send(w4, 3)
+            share((3, 1), (3, 3))
+
+        def e10():
+            arrived((0, 2))
+            share((0, 2))
+
+        def e11():
+            hidden_next(3)
+            arrived((2, 1), (2, 3))
+            send(w4, 2)
+            share((2, 1), (2, 3))
+
+        def last(d1):
+            arrived((d1, 2))
+            share((d1, 2))
+
+        at(1, e1)
+        at(2, lambda: send(w3, 1))
+        at(3, e3)
+        at(4, lambda: send(w3, 3))
+        at(5, e5)
+        at(6, e6)
         at(7, lambda: hidden_next(2))
-        at(9, w_step4)
-        at(11, lambda: hidden_next(3))
-        at(12, w_step5)
-        at(15, w_step6)
+        at(8, e8)
+        at(9, e9)
+        at(10, e10)
+        at(11, e11)
+        at(12, lambda: last(1))
+        at(13, lambda: last(3))
+        at(14, lambda: last(2))
 
     def chunk(j, carry):
         for k in range(1, 4):
@@ -366,11 +385,13 @@
     return centred * lax.rsqrt(variance + 1e-05) * gain + shift
 
 
-FC = 512
-RB = 256
-
-
-def feed_kernel(info_ref, att_ref, tok_ref, wo_ref, vec_ref, up_ref, dn_ref, out_ref, tot_ref, normed, acc):
+FC = 1024
+RB = 512
+
+
+def feed_kernel(
+    len_ref, att_ref, tok_ref, wo_ref, g1_ref, b1_ref, g2_ref, b2_ref, up_ref, dn_ref, out_ref, tot_ref, normed, acc
+):
     i = pl.program_id(0)
 
     @pl.when(i == 0)
@@ -379,7 +400,7 @@
             rows = pl.ds(r * RB, RB)
             mixed = jnp.dot(att_ref[rows, :], wo_ref[...], preferred_element_type=F32)
             mixed = mixed + tok_ref[rows, :].astype(F32)
-            n = layer_norm(mixed, vec_ref[0:1, :], vec_ref[1:2, :]).astype(BF)
+            n = layer_norm(mixed, g1_ref[...], b1_ref[...]).astype(BF)
             normed[rows, :] = n
             acc[rows, :] = n.astype(F32)
 
@@ -396,15 +417,15 @@
         total = jnp.zeros((1, 1024), F32)
         for r in range(512 // RB):
             rows = pl.ds(r * RB, RB)
-            final = layer_norm(acc[rows, :], vec_ref[2:3, :], vec_ref[3:4, :])
+            final = layer_norm(acc[rows, :], g2_ref[...], b2_ref[...])
             out_ref[rows, :] = final.astype(BF)
-            pos = lax.broadcasted_iota(jnp.int32, (RB, 1), 0) + (info_ref[1] + r * RB)
-            valid = (pos < info_ref[0]).astype(F32)
+            pos = lax.broadcasted_iota(jnp.int32, (RB, 1), 0) + (lax.axis_index("seq") * 512 + r * RB)
+            valid = (pos < len_ref[0]).astype(F32)
             total = total + jnp.sum(final * valid, axis=0, keepdims=True)
         tot_ref[...] = total
 
 
-def feed(info, att, tokens, output_weight, vecs, wf):
+def feed(lengths, att, tokens, output_weight, rows, wf):
     whole = lambda shape: pl.BlockSpec(shape, lambda i: (0,) * len(shape))
     return pl.pallas_call(
         feed_kernel,
@@ -416,7 +437,7 @@
             whole((512, 1024)),
             whole((512, 1024)),
             whole((1024, 1024)),
-            whole((4, 1024)),
+            *[whole((1, 1024))] * 4,
             pl.BlockSpec((1, 1024, FC), lambda i: (0, 0, i)),
             pl.BlockSpec((1, 1024, FC), lambda i: (1, 0, i)),
         ],
@@ -425,7 +446,7 @@
         compiler_params=pltpu.CompilerParams(
             dimension_semantics=("arbitrary",), vmem_limit_bytes=56 * 2**20
         ),
-    )(info, att, tokens, output_weight, vecs, wf, wf)
+    )(lengths, att, tokens, output_weight, *rows, wf, wf)
 
 
 def loss_kernel(len_ref, pos_ref, tot_ref, q_ref, emb_ref, loss_ref, parts, sent, passages, ssem, rsem, ssem2, rsem2):
@@ -469,11 +490,11 @@
     rows = [emb] + [passages[d] for d in range(1, 16)]
     allp = jnp.concatenate(rows, axis=0).astype(BF)
     logits = 20.0 * lax.dot_general(
-        short_q, allp, (((1,), (1,)), ((), ())), preferred_element_type=F32
+        allp, short_q, (((1,), (1,)), ((), ())), preferred_element_type=F32
     )
-    ids = lax.rem(g + 16 - lax.broadcasted_iota(jnp.int32, (8, 16), 1), 16)
-    picked = jnp.sum(jnp.where(pos_ref[...] == ids, logits, 0.0), axis=1, keepdims=True)
-    loss_ref[...] = jnp.log(jnp.sum(jnp.exp(logits), axis=1, keepdims=True)) - picked
+    ids = lax.rem(g + 16 - lax.broadcasted_iota(jnp.int32, (16, 8), 0), 16)
+    picked = jnp.sum(jnp.where(pos_ref[...] == ids, logits, 0.0), axis=0, keepdims=True)
+    loss_ref[...] = jnp.log(jnp.sum(jnp.exp(logits), axis=0, keepdims=True)) - picked
     for cp in first + second:
         cp.wait_send()
 
@@ -484,7 +505,7 @@
     return pl.pallas_call(
         loss_kernel,
         name="losses",
-        out_shape=(jax.ShapeDtypeStruct((1, 1024), F32), jax.ShapeDtypeStruct((8, 1), F32)),
+        out_shape=(jax.ShapeDtypeStruct((1, 1024), F32), jax.ShapeDtypeStruct((1, 8), F32)),
         in_specs=[pl.BlockSpec(memory_space=pltpu.SMEM), vm, vm, vm],
         out_specs=(vm, vm),
         scratch_shapes=[
@@ -503,11 +524,10 @@
 ):
     tokens = hidden_in[0]
     att, wf = attend(lengths, tokens, project_weight, up_weight, down_weight)
-    vecs = jnp.stack([first_gain, first_shift, second_gain, second_shift])
-    info = jnp.concatenate([lengths, (lax.axis_index("seq") * 512)[None].astype(jnp.int32)])
-    final, total = feed(info, att, tokens, output_weight, vecs, wf)
-    embedding, loss = losses(lengths, positive[:, None], total, queries)
-    return final[None], embedding, loss[:, 0]
+    rows = [v[None, :] for v in (first_gain, first_shift, second_gain, second_shift)]
+    final, total = feed(lengths, att, tokens, output_weight, rows, wf)
+    embedding, loss = losses(lengths, positive[None, :], total, queries)
+    return final[None], embedding, loss[0]
 
 
 def solution(mesh):

time: 113 us -> 105 us (0.929)
  Pallas kernels: 106 us -> 101 us
  other arithmetic: 2.57 us -> 0 us
    pallas_call x1, Pallas kernels: 75.8 us -> 71 us  [attend(): pl.pallas_call(attend_kernel, name='attend', out_shape=(jax.ShapeDtypeStr...]
    pallas_call x1, Pallas kernels: 18.7 us -> 16.8 us  [feed(): pl.pallas_call(feed_kernel, name='feed', grid=(4096 // FC,), out_shape=(j...]
    pallas_call x1, Pallas kernels: 11.6 us -> 13.2 us  [losses(): pl.pallas_call(loss_kernel, name='losses', out_shape=(jax.ShapeDtypeStruc...]
    pallas_call x1 -> x0, other arithmetic: 1.3 us -> none  [losses(): pl.pallas_call(loss_kernel, name='losses', out_shape=(jax.ShapeDtypeStruc...]
    unnamed x11 -> x2, local copies, waits for them, and re-layouts: 1.29 us -> 2.42 us
where the time goes in v2:
time: 105 us
  Pallas kernels  101 us (96%)
  local copies, waits for them, and re-layouts  2.42 us (2%)
  between operations  1.29 us (1%)
    pallas_call x1, Pallas kernels, attend(): pl.pallas_call(attend_kernel, name='attend', out_shape=(jax.ShapeDtypeStr...  71 us
    pallas_call x1, Pallas kernels, feed(): pl.pallas_call(feed_kernel, name='feed', grid=(4096 // FC,), out_shape=(j...  16.8 us
    pallas_call x1, Pallas kernels, losses(): pl.pallas_call(loss_kernel, name='losses', out_shape=(jax.ShapeDtypeStruc...  13.2 us
    unnamed x2, local copies, waits for them, and re-layouts  2.42 us

profile of v2, /device:TPU:1, one launch (start us, length us, event | category | flops | bytes accessed | tf_op | source)
XLA Modules:
  0.0 104.7 jit_solution(16459032447877580766)
XLA Ops:
  1.3 71.0 %attend.1 = (bf16[512,1024]{1,0:T(8,128)(2,1)}, bf16[2,1024,4096]{2,1,0:T(8,128)(2,1)}) custom-call(s32[1]{0:T(128)S(6)} %copy.17.len_ref, bf16[512,1024]{1,0:T(8,128)(2,1)} %bitcast.8, bf16[1024,3072]{1,0:T(8,128)(2,1)} %w_ref.1, bf16[64,4096]{1,0:T(8,128)(2,1)} %up_ref.1, bf16[64,4096]{1,0:T(8,128)(2,1)} %dn_ref.1), custom_call_target="tpu_custom_call" | custom-call | tf_op jit(solution)/shard_map/attend/pallas_call | solution.py:350
  72.3 16.8 %feed.1 = (bf16[512,1024]{1,0:T(8,128)(2,1)}, f32[1,1024]{1,0:T(1,128)}) custom-call(s32[1]{0:T(128)S(6)} %copy.17.len_ref, bf16[512,1024]{1,0:T(8,128)(2,1)} %get-tuple-element.9.att_ref, bf16[512,1024]{1,0:T(8,128)(2,1)} %bitcast.9, bf16[1024,1024]{1,0:T(8,128)(2,1)} %wo_ref.1, f32[1,1024]{1,0:T(1,128)} %bitcast.10, f32[1,1024]{1,0:T(1,128)} %bitcast.11, ...), custom_call_target="tpu_custom_call" | custom-call | tf_op jit(solution)/shard_map/feed/pallas_call | solution.py:430
  89.1 13.2 %losses.1 = (f32[1,1024]{1,0:T(1,128)}, f32[1,8]{1,0:T(1,128)}) custom-call(s32[1]{0:T(128)S(6)} %copy.17.len_ref, s32[1,8]{1,0:T(1,128)} %bitcast.14, f32[1,1024]{1,0:T(1,128)} %get-tuple-element.12.tot_ref, f32[8,1024]{1,0:T(8,128)} %q_ref.1), custom_call_target="tpu_custom_call" | custom-call | tf_op jit(solution)/shard_map/losses/pallas_call | solution.py:505
  102.3 1.3 %copy.18 = f32[1,1024]{1,0:T(1,128)} copy(f32[1,1024]{1,0:T(1,128)} %get-tuple-element.19) | data formatting | bytes 8192
  103.6 1.1 %copy.19 = f32[8]{0:T(128)} copy(f32[8]{0:T(128)} %bitcast.16) | data formatting | bytes 64

commit v3 on v2

--- a/solution.py
+++ b/solution.py
@@ -13,17 +13,14 @@
 F32 = jnp.float32
 NEG = -1e30
 KB = 1024
-QT = 512
-NT = 1024 // QT
-TILES = 8 * NT
-U = 4
-ITERS = TILES // U
+RS = 256
+EV = (3, 3, 6, 6, 14, 14, 14, 18, 18, 22, 25, 28, 28, 30)
 SCALE = math.log2(math.e) / 8.0
 
 
 def attend_kernel(
     len_ref, x_ref, w_ref, up_ref, dn_ref, att_ref, wf_ref,
-    xbuf, wqkv, kscr, vscr, qscr, acc, mx, s_a, s_b, al, stage, wv,
+    xbuf, wqkv, kscr, vscr, qscr, acc, mx, sbuf, al, stage, wv,
     lsem, hs, hr, ds, dr, ws, wr, ps, pr, osem,
 ):
     s = lax.axis_index("seq")
@@ -155,22 +152,34 @@
             h = 4 * i + u
             qscr[h, (u % 2) * 64 : (u % 2) * 64 + 64, :] = qt[64 * u : 64 * u + 64]
 
-    bufs = [s_a, s_b]
-
-    def scores(h, t, sref, slot):
-        sl = pl.ds(pl.multiple_of(t * QT, QT), QT)
-        sc = jnp.dot(kscr[h // 2], qscr[h, :, sl], preferred_element_type=F32)
-        sref[...] = sc
-        old = mx[h, :, sl]
-        new = jnp.maximum(old, jnp.max(sc, axis=0, keepdims=True))
-        mx[h, :, sl] = new
-        al[slot] = jnp.exp2(old - new)
-        al[slot + 2] = new
-
-    def values(h, t, sref, slot):
-        sl = pl.ds(pl.multiple_of(t * QT, QT), QT)
-        p = jnp.exp2(sref[...] - al[slot + 2]).astype(BF)
-        acc[h, :, sl] = acc[h, :, sl] * al[slot] + jnp.dot(vscr[h], p, preferred_element_type=F32)
+    def score_rows(h, r):
+        rows = pl.ds(r * RS, RS)
+        sc = jnp.dot(kscr[h // 2, rows, :], qscr[h], preferred_element_type=F32)
+        sbuf[rows, :] = sc
+        return jnp.max(sc.reshape(RS // 8, 8, 1024), axis=0)
+
+    def new_max(h, tops):
+        top = functools.reduce(jnp.maximum, tops)
+        old = mx[h]
+        new = jnp.maximum(old, jnp.max(top, axis=0, keepdims=True))
+        mx[h] = new
+        al[0] = jnp.exp2(old - new)
+        al[1] = new
+
+    def head_step(h, following):
+        factor = al[0]
+        top = al[1]
+        tops = []
+        out = None
+        for r in range(KB // RS):
+            p = jnp.exp2(sbuf[pl.ds(r * RS, RS), :] - top).astype(BF)
+            if following is not None:
+                tops.append(score_rows(following, r))
+            part = jnp.dot(vscr[h, :, pl.ds(r * RS, RS)], p, preferred_element_type=F32)
+            out = part if out is None else out + part
+        if following is not None:
+            new_max(following, tops)
+        acc[h] = acc[h] * factor + out
 
     def events(e):
         def at(k, fn):
@@ -225,7 +234,6 @@
             send(w2)
 
         def e3():
-            hidden_next(1)
             share((1, 0), (3, 0))
 
         def e5():
@@ -253,7 +261,6 @@
             share((0, 2))
 
         def e11():
-            hidden_next(3)
             arrived((2, 1), (2, 3))
             send(w4, 2)
             share((2, 1), (2, 3))
@@ -262,20 +269,22 @@
             arrived((d1, 2))
             share((d1, 2))
 
-        at(1, e1)
-        at(2, lambda: send(w3, 1))
-        at(3, e3)
-        at(4, lambda: send(w3, 3))
-        at(5, e5)
-        at(6, e6)
-        at(7, lambda: hidden_next(2))
-        at(8, e8)
-        at(9, e9)
-        at(10, e10)
-        at(11, e11)
-        at(12, lambda: last(1))
-        at(13, lambda: last(3))
-        at(14, lambda: last(2))
+        at(EV[0], e1)
+        at(EV[1], lambda: send(w3, 1))
+        at(EV[2], e3)
+        at(EV[3], lambda: send(w3, 3))
+        at(EV[4], e5)
+        at(EV[5], e6)
+        at(12, lambda: hidden_next(2))
+        at(5, lambda: hidden_next(1))
+        at(20, lambda: hidden_next(3))
+        at(EV[7], e8)
+        at(EV[8], e9)
+        at(EV[9], e10)
+        at(EV[10], e11)
+        at(EV[11], lambda: last(1))
+        at(EV[12], lambda: last(3))
+        at(EV[13], lambda: last(2))
 
     def chunk(j, carry):
         for k in range(1, 4):
@@ -304,18 +313,15 @@
             for u in range(4):
                 vscr[4 * i + u, 0:64, :] = vt[64 * u : 64 * u + 64]
 
-        scores(0, 0, s_a, 0)
-
-        def it(k, carry2):
-            events(j * ITERS + k)
-            for u in range(U):
-                i = k * U + u
-                nx = jnp.minimum(i + 1, TILES - 1)
-                scores(nx // NT, lax.rem(nx, NT), bufs[(u + 1) % 2], (u + 1) % 2)
-                values(i // NT, i % NT, bufs[u % 2], u % 2)
+        new_max(0, [score_rows(0, r) for r in range(KB // RS)])
+
+        def it(h, carry2):
+            events(j * 8 + h)
+            head_step(h, h + 1)
             return carry2
 
-        lax.fori_loop(0, ITERS, it, 0)
+        lax.fori_loop(0, 7, it, 0)
+        head_step(7, None)
         return carry
 
     lax.fori_loop(0, 4, chunk, 0)
@@ -364,9 +370,8 @@
             pltpu.VMEM((8, 256, 1024), BF),
             pltpu.VMEM((8, 80, 1024), F32),
             pltpu.VMEM((8, 1, 1024), F32),
-            pltpu.VMEM((KB, QT), F32),
-            pltpu.VMEM((KB, QT), F32),
-            pltpu.VMEM((4, 1, QT), F32),
+            pltpu.VMEM((KB, 1024), F32),
+            pltpu.VMEM((2, 1, 1024), F32),
             pltpu.VMEM((1024, 512), BF),
             pltpu.VMEM((2, 64, 4096), BF),
             dma((8,)), dma((6,)), dma((6,)), dma((7,)), dma((7,)),

time: 105 us -> 102 us (0.971)
  Pallas kernels: 101 us -> 98 us
    pallas_call x1, Pallas kernels: 71 us -> 68.6 us  [attend(): pl.pallas_call(attend_kernel, name='attend', out_shape=(jax.ShapeDtypeStr...]
where the time goes in v3:
time: 102 us
  Pallas kernels  98 us (96%)
  local copies, waits for them, and re-layouts  2.42 us (2%)
  between operations  1.29 us (1%)
    pallas_call x1, Pallas kernels, attend(): pl.pallas_call(attend_kernel, name='attend', out_shape=(jax.ShapeDtypeStr...  68.6 us
    pallas_call x1, Pallas kernels, feed(): pl.pallas_call(feed_kernel, name='feed', grid=(4096 // FC,), out_shape=(j...  16.8 us
    pallas_call x1, Pallas kernels, losses(): pl.pallas_call(loss_kernel, name='losses', out_shape=(jax.ShapeDtypeStruc...  12.6 us
    unnamed x2, local copies, waits for them, and re-layouts  2.42 us

profile of v3, /device:TPU:1, one launch (start us, length us, event | category | flops | bytes accessed | tf_op | source)
XLA Modules:
  0.0 101.7 jit_solution(8448636868925622464)
XLA Ops:
  1.3 68.6 %attend.1 = (bf16[512,1024]{1,0:T(8,128)(2,1)}, bf16[2,1024,4096]{2,1,0:T(8,128)(2,1)}) custom-call(s32[1]{0:T(128)S(6)} %copy.17.len_ref, bf16[512,1024]{1,0:T(8,128)(2,1)} %bitcast.8, bf16[1024,3072]{1,0:T(8,128)(2,1)} %w_ref.1, bf16[64,4096]{1,0:T(8,128)(2,1)} %up_ref.1, bf16[64,4096]{1,0:T(8,128)(2,1)} %dn_ref.1), custom_call_target="tpu_custom_call" | custom-call | tf_op jit(solution)/shard_map/attend/pallas_call | solution.py:356
  69.8 16.8 %feed.1 = (bf16[512,1024]{1,0:T(8,128)(2,1)}, f32[1,1024]{1,0:T(1,128)}) custom-call(s32[1]{0:T(128)S(6)} %copy.17.len_ref, bf16[512,1024]{1,0:T(8,128)(2,1)} %get-tuple-element.9.att_ref, bf16[512,1024]{1,0:T(8,128)(2,1)} %bitcast.9, bf16[1024,1024]{1,0:T(8,128)(2,1)} %wo_ref.1, f32[1,1024]{1,0:T(1,128)} %bitcast.10, f32[1,1024]{1,0:T(1,128)} %bitcast.11, ...), custom_call_target="tpu_custom_call" | custom-call | tf_op jit(solution)/shard_map/feed/pallas_call | solution.py:435
  86.6 12.6 %losses.1 = (f32[1,1024]{1,0:T(1,128)}, f32[1,8]{1,0:T(1,128)}) custom-call(s32[1]{0:T(128)S(6)} %copy.17.len_ref, s32[1,8]{1,0:T(1,128)} %bitcast.14, f32[1,1024]{1,0:T(1,128)} %get-tuple-element.12.tot_ref, f32[8,1024]{1,0:T(8,128)} %q_ref.1), custom_call_target="tpu_custom_call" | custom-call | tf_op jit(solution)/shard_map/losses/pallas_call | solution.py:510
  99.2 1.3 %copy.18 = f32[1,1024]{1,0:T(1,128)} copy(f32[1,1024]{1,0:T(1,128)} %get-tuple-element.19) | data formatting | bytes 8192
  100.5 1.1 %copy.19 = f32[8]{0:T(128)} copy(f32[8]{0:T(128)} %bitcast.16) | data formatting | bytes 64

commit v4 on v3

--- a/solution.py
+++ b/solution.py
@@ -14,7 +14,7 @@
 NEG = -1e30
 KB = 1024
 RS = 256
-EV = (3, 3, 6, 6, 14, 14, 14, 18, 18, 22, 25, 28, 28, 30)
+EV = (2, 2, 2, 2, 11, 11, 14, 18, 18, 25, 25, 30, 30, 30)
 SCALE = math.log2(math.e) / 8.0
 
 

time: 102 us -> 99.6 us (0.976)
  Pallas kernels: 98 us -> 95.7 us
    pallas_call x1, Pallas kernels: 68.6 us -> 66.3 us  [attend(): pl.pallas_call(attend_kernel, name='attend', out_shape=(jax.ShapeDtypeStr...]
where the time goes in v4:
time: 99.6 us; the launch traced here: 99.4 us
  Pallas kernels  95.7 us (96%)
  local copies, waits for them, and re-layouts  2.42 us (2%)
  between operations  1.29 us (1%)
    pallas_call x1, Pallas kernels, attend(): pl.pallas_call(attend_kernel, name='attend', out_shape=(jax.ShapeDtypeStr...  66.3 us
    pallas_call x1, Pallas kernels, feed(): pl.pallas_call(feed_kernel, name='feed', grid=(4096 // FC,), out_shape=(j...  16.8 us
    pallas_call x1, Pallas kernels, losses(): pl.pallas_call(loss_kernel, name='losses', out_shape=(jax.ShapeDtypeStruc...  12.7 us
    unnamed x2, local copies, waits for them, and re-layouts  2.42 us

profile of v4, /device:TPU:1, one launch (start us, length us, event | category | flops | bytes accessed | tf_op | source)
XLA Modules:
  0.0 99.4 jit_solution(2583107858150544767)
XLA Ops:
  1.3 66.3 %attend.1 = (bf16[512,1024]{1,0:T(8,128)(2,1)}, bf16[2,1024,4096]{2,1,0:T(8,128)(2,1)}) custom-call(s32[1]{0:T(128)S(6)} %copy.17.len_ref, bf16[512,1024]{1,0:T(8,128)(2,1)} %bitcast.8, bf16[1024,3072]{1,0:T(8,128)(2,1)} %w_ref.1, bf16[64,4096]{1,0:T(8,128)(2,1)} %up_ref.1, bf16[64,4096]{1,0:T(8,128)(2,1)} %dn_ref.1), custom_call_target="tpu_custom_call" | custom-call | tf_op jit(solution)/shard_map/attend/pallas_call | solution.py:356
  67.5 16.8 %feed.1 = (bf16[512,1024]{1,0:T(8,128)(2,1)}, f32[1,1024]{1,0:T(1,128)}) custom-call(s32[1]{0:T(128)S(6)} %copy.17.len_ref, bf16[512,1024]{1,0:T(8,128)(2,1)} %get-tuple-element.9.att_ref, bf16[512,1024]{1,0:T(8,128)(2,1)} %bitcast.9, bf16[1024,1024]{1,0:T(8,128)(2,1)} %wo_ref.1, f32[1,1024]{1,0:T(1,128)} %bitcast.10, f32[1,1024]{1,0:T(1,128)} %bitcast.11, ...), custom_call_target="tpu_custom_call" | custom-call | tf_op jit(solution)/shard_map/feed/pallas_call | solution.py:435
  84.3 12.7 %losses.1 = (f32[1,1024]{1,0:T(1,128)}, f32[1,8]{1,0:T(1,128)}) custom-call(s32[1]{0:T(128)S(6)} %copy.17.len_ref, s32[1,8]{1,0:T(1,128)} %bitcast.14, f32[1,1024]{1,0:T(1,128)} %get-tuple-element.12.tot_ref, f32[8,1024]{1,0:T(8,128)} %q_ref.1), custom_call_target="tpu_custom_call" | custom-call | tf_op jit(solution)/shard_map/losses/pallas_call | solution.py:510
  97.0 1.3 %copy.18 = f32[1,1024]{1,0:T(1,128)} copy(f32[1,1024]{1,0:T(1,128)} %get-tuple-element.19) | data formatting | bytes 8192
  98.3 1.1 %copy.19 = f32[8]{0:T(128)} copy(f32[8]{0:T(128)} %bitcast.16) | data formatting | bytes 64
